TPU v7x, 32 devices: a whole 2x2x4 slice. The times are simulated.
32 devices in a mesh: dp: 8 (over z, y), mp: 4 (over x, core).
Axes of the slice: x: 2, y: 2, z: 4, core: 2. Of those that a mesh axis runs over, the one named last changes fastest.
Arguments:
- tokens: bfloat16 [2048, 4096], P('dp', 'mp'), may hold values from -6 to 6
- router_weight: bfloat16 [4096, 64], P('mp'), may hold values from -1 to 1
- valid_count: int32 [8], P('dp'), may hold values from 64 to 256, as said below
- expert_id: int32 [2048], P('dp'), may hold values from 0 to 63, as said below
- slot_id: int32 [2048], P('dp'), may hold values from 0 to 5
Outputs:
- gates: float32 [2048], P('dp')
- dispatched: bfloat16 [384, 8, 4096], P('dp', None, 'mp')
Inputs may be any that keep to these rules, and one draw needn't show every extreme that they name: Group g's live tokens are its first valid_count[g] positions; the last group is full. Within one group no two positions share an expert and a slot. Flat slots expert_id * 6 + slot_id are held 48 in a row by one owner; one group's positions take at most 32 slots of any owner, and in every group some owner has 32 of its slots taken by live tokens.
All inputs are finite; a program needn't handle non-finite values.
Results may differ from a plain program's by a relative error of at most 0.001.
Values may be sent and summed in bfloat16 or wider, within the bound.
A program may use at most 64 MiB of HBM per device.

v0:
```python
import jax
import jax.numpy as jnp
from jax import lax
from jax.sharding import PartitionSpec as P

E = 64
ITERS = 5
CAP = 6


def dispatch(tokens, live, expert_id, slot_id):
    total_slots = E * CAP
    target = expert_id * CAP + slot_id
    placed = jnp.where(live, target, total_slots)
    buffer = (
        jnp.zeros((total_slots, tokens.shape[1]), jnp.bfloat16).at[placed].set(tokens, mode="drop")
    )
    return lax.all_to_all(buffer[:, None, :], "dp", split_axis=0, concat_axis=1, tiled=True)


def balance(logits, live, expert_id, total, column_sum):
    experts = logits.shape[1]
    affinity = jnp.exp(logits)
    weight = live.astype(jnp.float32)
    col_scale = jnp.ones((experts,), jnp.float32)
    row_scale = jnp.ones((logits.shape[0],), jnp.float32)
    for sweep in range(ITERS):
        row_scale = experts / jnp.sum(affinity * col_scale[None, :], axis=1)
        column = column_sum(jnp.sum(affinity * (weight * row_scale)[:, None], axis=0))
        col_scale = total / column
    chosen = expert_id[:, None] == jnp.arange(experts, dtype=jnp.int32)[None, :]
    picked = jnp.sum(jnp.where(chosen, affinity * col_scale[None, :], 0.0), axis=1)
    return weight * row_scale * picked


def local(tokens, router_weight, valid_count, expert_id, slot_id):
    rows = tokens.shape[0]
    live = jnp.arange(rows, dtype=jnp.int32) < valid_count[0]
    dispatched = None
    total = lax.psum(valid_count.astype(jnp.float32)[0], "dp")
    partial_logits = jnp.dot(tokens, router_weight, preferred_element_type=jnp.float32)
    logits = lax.psum(partial_logits, "mp")

    def group_sum(partial_value):
        return lax.psum(partial_value, "dp")

    gates = balance(logits, live, expert_id, total, group_sum)
    dispatched = dispatch(tokens, live, expert_id, slot_id)
    return (gates, dispatched)


def solution(mesh):
    placed = (P("dp", "mp"), P("mp", None), P("dp"), P("dp"), P("dp"))
    return jax.shard_map(
        local, mesh=mesh, in_specs=placed, out_specs=(P("dp"), P("dp", None, "mp")), check_vma=False
    )
```

profile of v0, /device:TPU:0, one launch (start us, length us, event | category | flops | bytes accessed | tf_op | source)
XLA Modules:
  0.0 163.1 jit_solution(8325949597759556054)
XLA Ops:
  7.2 0.8 copy-done
  8.1 1.9 %fusion.2 = f32[256,64]{0,1:T(8,128)} fusion(bf16[256,1024]{1,0:T(8,128)(2,1)} %param.5, bf16[1024,64]{0,1:T(8,128)(2,1)S(1)} %copy-done), kind=kOutput, calls=%fused_computation.27 | convolution fusion | flops 33554432 | bytes 720896 | tf_op jit(solution)/shard_map/dot_general | solution.py:41
  11.4 2.4 %scatter_custom_fusion = bf16[384,1024]{1,0:T(8,128)(2,1)S(1)} fusion(s32[256]{0:T(256)S(1)} %compare_select_fusion, bf16[256,1024]{1,0:T(8,128)(2,1)} %param.5, bf16[]{:T(256)} %constant.14.clone.1), kind=kCustom, calls=%fused_computation.1 | custom fusion | bytes 786944 | tf_op jit(solution)/shard_map/scatter | solution.py:16
  14.3 1.2 reduce
  15.6 1.5 reshape.53
  17.0 7.3 %all-to-all-start = ((bf16[8,2,24576]{2,1,0:T(2,128)(2,1)}), bf16[8,2,24576]{2,1,0:T(2,128)(2,1)S(1)}, u32[]{:S(2)}, u32[]{:S(2)}) async-start(bf16[8,2,24576]{2,1,0:T(2,128)(2,1)} %reshape.53), calls=%async_computation | async-start | bytes 1572864 | tf_op jit(solution)/shard_map/all_to_all | solution.py:18
  24.3 20.2 %all-reduce.3.cloned.1.call-done = f32[256,64]{0,1:T(8,128)} async-done(((f32[256,64]{0,1:T(8,128)}), f32[256,64]{0,1:T(8,128)}) %all-reduce.3.cloned.1.call-update) | async-done | bytes 65552 | tf_op jit(solution)/shard_map/psum | solution.py:42
  44.6 0.9 exponential_reduce_fusion
  45.4 1.0 multiply_reduce_fusion.8
  46.4 22.5 %all-reduce = (f32[64]{0:T(128)S(1)}, f32[]{:T(128)}) all-reduce(f32[64]{0:T(128)S(1)} %multiply_reduce_fusion.8, f32[]{:T(128)} %bitcast.1), channel_id=1, replica_groups=mesh['dp'=8,'mp'=4] {'dp'}, use_global_device_ids=true, to_apply=%region_4.0 | all-reduce | flops 65 | bytes 520 | tf_op jit(solution)/shard_map/psum | solution.py:45
  69.6 0.9 multiply_reduce_fusion.7
  70.5 1.0 multiply_reduce_fusion.6
  71.5 17.1 %psum.52 = f32[64]{0:T(128)S(1)} all-reduce(f32[64]{0:T(128)S(1)} %multiply_reduce_fusion.6), channel_id=1, replica_groups=mesh['dp'=8,'mp'=4] {'dp'}, use_global_device_ids=true, to_apply=%region_7.0 | all-reduce | flops 64 | bytes 512 | tf_op jit(solution)/shard_map/psum | solution.py:45
  89.3 0.9 multiply_reduce_fusion.5
  90.2 1.0 multiply_reduce_fusion.4
  91.2 19.1 %psum.53 = f32[64]{0:T(128)S(1)} all-reduce(f32[64]{0:T(128)S(1)} %multiply_reduce_fusion.4), channel_id=1, replica_groups=mesh['dp'=8,'mp'=4] {'dp'}, use_global_device_ids=true, to_apply=%region_10.0 | all-reduce | flops 64 | bytes 512 | tf_op jit(solution)/shard_map/psum | solution.py:45
  111.0 0.9 multiply_reduce_fusion.3
  111.9 1.0 multiply_reduce_fusion.2
  112.9 17.1 %psum.54 = f32[64]{0:T(128)S(1)} all-reduce(f32[64]{0:T(128)S(1)} %multiply_reduce_fusion.2), channel_id=1, replica_groups=mesh['dp'=8,'mp'=4] {'dp'}, use_global_device_ids=true, to_apply=%region_13.0 | all-reduce | flops 64 | bytes 512 | tf_op jit(solution)/shard_map/psum | solution.py:45
  130.7 0.9 multiply_reduce_fusion.1
  131.6 1.0 multiply_reduce_fusion
  132.6 19.1 %psum.55 = f32[64]{0:T(128)S(1)} all-reduce(f32[64]{0:T(128)S(1)} %multiply_reduce_fusion), channel_id=1, replica_groups=mesh['dp'=8,'mp'=4] {'dp'}, use_global_device_ids=true, to_apply=%region_16.0 | all-reduce | flops 64 | bytes 512 | tf_op jit(solution)/shard_map/psum | solution.py:45
  152.4 0.9 select_reduce_fusion
  155.0 1.3 copy.9
  (21 shorter events, 6.2 us)
Async XLA Ops:
  7.2 0.9 copy-start
  7.2 37.4 %all-reduce.3.cloned.1.call-start = ((), (), s32[]{:S(2)}) async-start(), calls=%async_computation.1 | async-start | bytes 131072 | tf_op jit(solution)/shard_map/psum | solution.py:42
  15.6 136.8 %copy-start.1 = (s32[256]{0:T(256)S(1)}, s32[256]{0:T(256)}, u32[]{:S(2)}) copy-start(s32[256]{0:T(256)} %param.8) | copy-start | bytes 3076
  17.0 136.9 %all-to-all-start = ((bf16[8,2,24576]{2,1,0:T(2,128)(2,1)}), bf16[8,2,24576]{2,1,0:T(2,128)(2,1)S(1)}, u32[]{:S(2)}, u32[]{:S(2)}) async-start(bf16[8,2,24576]{2,1,0:T(2,128)(2,1)} %reshape.53), calls=%async_computation | async-start | bytes 1572864 | tf_op jit(solution)/shard_map/all_to_all | solution.py:18
Sparse Core Ops, SparseCore 0:
  10.3 34.2 all-reduce.2
where the time goes:
time: 164 us; the launch traced here: 163 us
  blocking collectives  95 us (58%)
  waiting for transfers between devices  20.3 us (12%)
  other arithmetic  16.1 us (10%)
  between operations  14.8 us (9%)
  local copies, waits for them, and re-layouts  7.63 us (5%)
  starting transfers between devices  7.35 us (4%)
  matrix products  1.95 us (1%)
    psum x5, blocking collectives, group_sum(): return lax.psum(partial_value, 'dp')  95 us
    psum x1, waiting for transfers between devices, local(): logits = lax.psum(partial_logits, 'mp')  20.2 us
    all_to_all x1, starting transfers between devices, dispatch(): lax.all_to_all(buffer[:, None, :], 'dp', split_axis=0, concat_axis=1, til...  7.31 us
    reduce_sum x5, other arithmetic, balance(): jnp.sum(affinity * (weight * row_scale)[:, None], axis=0)  4.8 us
    unnamed x8, local copies, waits for them, and re-layouts  4.71 us
    reduce_sum x5, other arithmetic, balance(): row_scale = experts / jnp.sum(affinity * col_scale[None, :], axis=1)  4.61 us
  transfers between devices with their start and end apart: 2, of which 1 were waited for; matrix products, arithmetic and copies ran while one was open for 13% of the time, Pallas kernels for 0%

commit v1 on v0

--- a/solution.py
+++ b/solution.py
@@ -39,7 +39,7 @@
     dispatched = None
     total = lax.psum(valid_count.astype(jnp.float32)[0], "dp")
     partial_logits = jnp.dot(tokens, router_weight, preferred_element_type=jnp.float32)
-    logits = lax.psum(partial_logits, "mp")
+    logits = jnp.sum(lax.all_gather(partial_logits, "mp"), axis=0)
 
     def group_sum(partial_value):
         return lax.psum(partial_value, "dp")

time: 164 us -> 125 us (0.76)
  waiting for transfers between devices: 20.3 us -> 0.01 us
  between operations: 14.8 us -> 1.46 us
  other arithmetic: 16.1 us -> 7.03 us
  blocking collectives: 95 us -> 101 us
  matrix products: 1.95 us -> 0.28 us
    psum x1 -> x0, waiting for transfers between devices: 20.2 us -> none  [local(): logits = lax.psum(partial_logits, 'mp')]
    all_gather x0 -> x1, blocking collectives: none -> 5.78 us  [local(): logits = jnp.sum(lax.all_gather(partial_logits, 'mp'), axis=0)]
    reduce_sum x5, other arithmetic: 4.8 us -> 0.58 us  [balance(): jnp.sum(affinity * (weight * row_scale)[:, None], axis=0)]
    reduce_sum x5, other arithmetic: 4.61 us -> 0.41 us  [balance(): row_scale = experts / jnp.sum(affinity * col_scale[None, :], axis=1)]
    dot_general x1, matrix products: 1.95 us -> 0.28 us  [local(): jnp.dot(tokens, router_weight, preferred_element_type=jnp.float32)]
    unnamed x8 -> x10, local copies, waits for them, and re-layouts: 4.71 us -> 3.87 us
  transfers between devices with their start and end apart: 2 -> 1, of which waited for: 1 -> 0; matrix products, arithmetic and copies ran while one was open for 13% -> 4% of each run, Pallas kernels for 0% -> 0%
where the time goes in v1:
time: 125 us; the launch traced here: 124 us
  blocking collectives  101 us (81%)
  starting transfers between devices  7.31 us (6%)
  other arithmetic  7.03 us (6%)
  local copies, waits for them, and re-layouts  6.91 us (6%)
  between operations  1.46 us (1%)
    psum x5, blocking collectives, group_sum(): return lax.psum(partial_value, 'dp')  95.6 us
    all_to_all x1, starting transfers between devices, dispatch(): lax.all_to_all(buffer[:, None, :], 'dp', split_axis=0, concat_axis=1, til...  7.31 us
    all_gather x1, blocking collectives, local(): logits = jnp.sum(lax.all_gather(partial_logits, 'mp'), axis=0)  5.78 us
    unnamed x10, local copies, waits for them, and re-layouts  3.87 us
    div x5, other arithmetic, balance(): col_scale = total / column  3.24 us
  transfers between devices with their start and end apart: 1, of which 0 were waited for; matrix products, arithmetic and copies ran while one was open for 4% of the time, Pallas kernels for 0%

profile of v1, /device:TPU:0, one launch (start us, length us, event | category | flops | bytes accessed | tf_op | source)
XLA Modules:
  0.0 124.4 jit_solution(14911172709928967846)
XLA Ops:
  1.3 0.7 compare_select_fusion
  2.0 2.4 %scatter_custom_fusion = bf16[384,1024]{1,0:T(8,128)(2,1)S(1)} fusion(s32[256]{0:T(256)S(1)} %compare_select_fusion, bf16[256,1024]{1,0:T(8,128)(2,1)} %param.5, bf16[]{:T(256)} %constant.14.clone.1), kind=kCustom, calls=%fused_computation.1 | custom fusion | bytes 786944 | tf_op jit(solution)/shard_map/scatter | solution.py:16
  4.4 0.5 broadcast.88
  5.0 1.2 reduce
  6.2 1.5 %reshape.54 = bf16[8,2,24576]{2,1,0:T(2,128)(2,1)} reshape(bf16[384,1024]{1,0:T(8,128)(2,1)S(1)} %reduce) | data formatting | bytes 1572864
  7.7 7.3 %all-to-all-start = ((bf16[8,2,24576]{2,1,0:T(2,128)(2,1)}), bf16[8,2,24576]{2,1,0:T(2,128)(2,1)S(1)}, u32[]{:S(2)}, u32[]{:S(2)}) async-start(bf16[8,2,24576]{2,1,0:T(2,128)(2,1)} %reshape.54), calls=%async_computation | async-start | bytes 1572864 | tf_op jit(solution)/shard_map/all_to_all | solution.py:18
  15.0 0.3 fusion.2
  15.3 5.8 %all-gather = f32[1024,64]{0,1:T(8,128)S(1)} all-gather(f32[256,64]{0,1:T(8,128)S(1)} %fusion.2), channel_id=2, replica_groups=mesh['dp'=8,'mp'=4] {'mp'}, dimensions={0}, use_global_device_ids=true | all-gather | bytes 327680 | tf_op jit(solution)/shard_map/all_gather | solution.py:42
  21.1 0.1 reshape.50
  21.2 0.2 reduce_sum.108
  21.5 23.1 %all-reduce = (f32[64]{0:T(128)S(1)}, f32[]{:T(128)}) all-reduce(f32[64]{0:T(128)S(1)} %multiply_reduce_fusion.8, f32[]{:T(128)} %bitcast.1), channel_id=1, replica_groups=mesh['dp'=8,'mp'=4] {'dp'}, use_global_device_ids=true, to_apply=%region_4.0 | all-reduce | flops 65 | bytes 520 | tf_op jit(solution)/shard_map/psum | solution.py:45
  44.6 0.6 broadcast_divide_fusion.4
  45.5 18.8 %psum.44 = f32[64]{0:T(128)S(1)} all-reduce(f32[64]{0:T(128)S(1)} %multiply_reduce_fusion.6), channel_id=1, replica_groups=mesh['dp'=8,'mp'=4] {'dp'}, use_global_device_ids=true, to_apply=%region_7.0 | all-reduce | flops 64 | bytes 512 | tf_op jit(solution)/shard_map/psum | solution.py:45
  64.3 0.6 broadcast_divide_fusion.3
  65.2 17.4 %psum.45 = f32[64]{0:T(128)S(1)} all-reduce(f32[64]{0:T(128)S(1)} %multiply_reduce_fusion.4), channel_id=1, replica_groups=mesh['dp'=8,'mp'=4] {'dp'}, use_global_device_ids=true, to_apply=%region_10.0 | all-reduce | flops 64 | bytes 512 | tf_op jit(solution)/shard_map/psum | solution.py:45
  82.6 0.6 broadcast_divide_fusion.2
  83.5 18.8 %psum.46 = f32[64]{0:T(128)S(1)} all-reduce(f32[64]{0:T(128)S(1)} %multiply_reduce_fusion.2), channel_id=1, replica_groups=mesh['dp'=8,'mp'=4] {'dp'}, use_global_device_ids=true, to_apply=%region_13.0 | all-reduce | flops 64 | bytes 512 | tf_op jit(solution)/shard_map/psum | solution.py:45
  102.3 0.6 broadcast_divide_fusion.1
  103.2 17.4 %psum.47 = f32[64]{0:T(128)S(1)} all-reduce(f32[64]{0:T(128)S(1)} %multiply_reduce_fusion), channel_id=1, replica_groups=mesh['dp'=8,'mp'=4] {'dp'}, use_global_device_ids=true, to_apply=%region_16.0 | all-reduce | flops 64 | bytes 512 | tf_op jit(solution)/shard_map/psum | solution.py:45
  120.7 0.6 broadcast_divide_fusion
  121.4 0.6 fusion.5
  122.0 0.8 reshape.55
  122.8 0.3 copy.10
  123.1 1.3 %copy.9 = bf16[48,8,1024]{2,1,0:T(8,128)(2,1)} copy(bf16[48,8,1024]{2,0,1:T(8,128)(2,1)S(1)} %bitcast.21) | data formatting | bytes 1572864
  (23 shorter events, 1.1 us)
Async XLA Ops:
  0.6 14.3 %copy-start = (bf16[1024,64]{0,1:T(8,128)(2,1)S(1)}, bf16[1024,64]{0,1:T(8,128)(2,1)}, u32[]{:S(2)}) copy-start(bf16[1024,64]{0,1:T(8,128)(2,1)} %param.6) | copy-start | bytes 393220
  6.2 8.8 %copy-start.1 = (bf16[256,1024]{1,0:T(8,128)(2,1)S(1)}, bf16[256,1024]{1,0:T(8,128)(2,1)}, u32[]{:S(2)}) copy-start(bf16[256,1024]{1,0:T(8,128)(2,1)} %param.5) | copy-start | bytes 1572868
  7.7 114.4 %all-to-all-start = ((bf16[8,2,24576]{2,1,0:T(2,128)(2,1)}), bf16[8,2,24576]{2,1,0:T(2,128)(2,1)S(1)}, u32[]{:S(2)}, u32[]{:S(2)}) async-start(bf16[8,2,24576]{2,1,0:T(2,128)(2,1)} %reshape.54), calls=%async_computation | async-start | bytes 1572864 | tf_op jit(solution)/shard_map/all_to_all | solution.py:18
  15.0 106.4 %copy-start.2 = (s32[256]{0:T(256)S(1)}, s32[256]{0:T(256)}, u32[]{:S(2)}) copy-start(s32[256]{0:T(256)} %param.8) | copy-start | bytes 3076
